TPU v7x, 32 devices: a whole 2x2x4 slice. The times are simulated.
32 devices in a mesh: zero: 4 (over y, x), width: 8 (over z, core).
Axes of the slice: x: 2, y: 2, z: 4, core: 2. Of those that a mesh axis runs over, the one named last changes fastest.
Arguments:
- train_gate: float32 [5120, 13824], P('zero', 'width'), may hold values from -0.125 to 0.125
- drift_gate: float32 [5120, 13824], P('zero', 'width'), may hold values from -0.078125 to 0.078125
- spread_gate: float32 [5120, 13824], P('zero', 'width'), may hold values from -0.078125 to 0.078125
- train_up: float32 [5120, 13824], P('zero', 'width'), may hold values from -0.125 to 0.125
- drift_up: float32 [5120, 13824], P('zero', 'width'), may hold values from -0.078125 to 0.078125
- spread_up: float32 [5120, 13824], P('zero', 'width'), may hold values from -0.078125 to 0.078125
- norm_gain: float32 [5120], P('zero'), may hold values from 0.25 to 1.75
Outputs:
- serving_gate: bfloat16 [5120, 13824], P(None, 'width')
- serving_up: bfloat16 [5120, 13824], P(None, 'width')
- factor_gate: float32 [13824], P('width')
- factor_up: float32 [13824], P('width')
All inputs are finite; a program needn't handle non-finite values. Where the computation divides by a largest or mean magnitude, that divisor is 1e-20 or more.
Results may differ from a plain program's by a relative error of at most 0.001.
Values may be sent and summed in bfloat16 or wider, within the bound.
A program may use at most 192 MiB of HBM per device.

v0:
```python
import jax
import jax.numpy as jnp
from jax import lax
from jax.sharding import PartitionSpec as P

learn_rate = 0.3
hold_rate = 0.9


def body(train_gate, drift_gate, spread_gate, train_up, drift_up, spread_up, norm_gain):
    hold_gate = hold_rate * drift_gate + spread_gate
    whole_gate = train_gate - learn_rate * hold_gate
    hold_up = hold_rate * drift_up + spread_up
    whole_up = train_up - learn_rate * hold_up
    whole_gained_gate = whole_gate * norm_gain[:, None]
    whole_gained_up = whole_up * norm_gain[:, None]
    factor_gate, factor_up = lax.pmax(
        (jnp.max(jnp.abs(whole_gained_gate), axis=0), jnp.max(jnp.abs(whole_gained_up), axis=0)),
        "zero",
    )
    narrow_gate, narrow_up = (
        (whole_gained_gate / factor_gate).astype(jnp.bfloat16),
        (whole_gained_up / factor_up).astype(jnp.bfloat16),
    )
    serving_gate, serving_up = (
        lax.all_gather(narrow_gate, "zero", axis=0, tiled=True),
        lax.all_gather(narrow_up, "zero", axis=0, tiled=True),
    )
    return (serving_gate, serving_up, factor_gate, factor_up)


def solution(mesh):
    return jax.shard_map(
        body,
        mesh=mesh,
        in_specs=(
            P("zero", "width"),
            P("zero", "width"),
            P("zero", "width"),
            P("zero", "width"),
            P("zero", "width"),
            P("zero", "width"),
            P("zero"),
        ),
        out_specs=(P(None, "width"), P(None, "width"), P("width"), P("width")),
        check_vma=False,
    )
```

profile of v0, /device:TPU:0, one launch (start us, length us, event | category | flops | bytes accessed | tf_op | source)
XLA Modules:
  0.0 420.9 jit_solution(3922969628244905731)
XLA Ops:
  7.2 0.0 all-gather.3.cloned.1.call-start
  7.2 24.5 %abs_reduce_fusion = (f32[1728]{0:T(1024)S(1)}, f32[1280,1728]{0,1:T(8,128)}, f32[1728]{0:T(1024)S(1)}, f32[1280,1728]{0,1:T(8,128)}) fusion(f32[1280]{0:T(1024)} %param.13, f32[1280,1728]{0,1:T(8,128)} %param.10, f32[1280,1728]{0,1:T(8,128)} %param.12, f32[1280,1728]{0,1:T(8,128)} %param.11, f32[1280,1728]{0,1:T(8,128)} %param.7, f32[1280,1728]{0,1:T(8,128)} %param.9, ...), kind=kLoop, calls=%fused_computation.1 | loop fusion | flops 30962304 | bytes 70797824 | tf_op jit(solution)/shard_map/reduce_max | solution.py:18
  31.7 17.5 %all-reduce = (f32[1728]{0:T(1024)S(1)}, f32[1728]{0:T(1024)S(1)}) all-reduce(f32[1728]{0:T(1024)S(1)} %get-tuple-element.10, f32[1728]{0:T(1024)S(1)} %get-tuple-element.6), channel_id=1, replica_groups=mesh['zero'=4,'width'=8] {'zero'}, use_global_device_ids=true, to_apply=%region_1.0 | all-reduce | flops 3456 | bytes 27648 | tf_op jit(solution)/shard_map/pmax | solution.py:17
  49.2 0.0 copy-start.1
  49.2 0.0 copy-start.2
  49.2 6.5 %divide_convert_fusion.1 = bf16[1280,1728]{0,1:T(8,128)(2,1)} fusion(f32[1280,1728]{0,1:T(8,128)} %get-tuple-element.11, f32[1728]{0:T(1024)S(1)} %get-tuple-element.18), kind=kLoop, calls=%fused_computation.3 | loop fusion | flops 4423680 | bytes 13277952 | tf_op jit(solution)/shard_map/convert_element_type | solution.py:22
  55.7 0.0 all-gather.3.cloned.1.call-update
  55.7 0.0 copy-done.1
  55.7 0.0 all-gather.5.cloned.1.call-start
  55.7 0.0 copy-done.2
  55.8 6.8 %divide_convert_fusion = bf16[1280,1728]{0,1:T(8,128)(2,1)} fusion(f32[1280,1728]{0,1:T(8,128)} %get-tuple-element.7, f32[1728]{0:T(1024)S(1)} %get-tuple-element.19), kind=kLoop, calls=%fused_computation | loop fusion | flops 4423680 | bytes 13277952 | tf_op jit(solution)/shard_map/convert_element_type | solution.py:23
  62.5 0.0 all-gather.5.cloned.1.call-update
  62.5 158.8 %all-gather.3.cloned.1.call-done = bf16[5120,1728]{0,1:T(8,128)(2,1)} async-done(((bf16[1280,1728]{0,1:T(8,128)(2,1)}), bf16[5120,1728]{0,1:T(8,128)(2,1)}) %all-gather.3.cloned.1.call-update) | async-done | bytes 17694736 | tf_op jit(solution)/shard_map/all_gather | solution.py:26
  221.3 168.6 %all-gather.5.cloned.1.call-done = bf16[5120,1728]{0,1:T(8,128)(2,1)} async-done(((bf16[1280,1728]{0,1:T(8,128)(2,1)}), bf16[5120,1728]{0,1:T(8,128)(2,1)}) %all-gather.5.cloned.1.call-update) | async-done | bytes 17694736 | tf_op jit(solution)/shard_map/all_gather | solution.py:27
  389.9 0.0 copy-start
  389.9 16.6 %copy.13 = bf16[5120,1728]{0,1:T(8,128)(2,1)} copy(bf16[5120,1728]{0,1:T(8,128)(2,1)} %all-gather.3.cloned.1.call-done) | data formatting | bytes 35389440
  406.5 1.1 copy-done
  407.6 6.5 %copy.14 = bf16[5120,1728]{0,1:T(8,128)(2,1)} copy(bf16[5120,1728]{0,1:T(8,128)(2,1)S(1)} %copy-done) | data formatting | bytes 35389440
Async XLA Ops:
  7.2 214.1 %all-gather.3.cloned.1.call-start = ((), (), s32[]{:S(2)}) async-start(), calls=%async_computation | async-start | bytes 22118400 | tf_op jit(solution)/shard_map/all_gather | solution.py:26
  49.2 6.5 %copy-start.1 = (f32[1728]{0:T(1024)}, f32[1728]{0:T(1024)S(1)}, u32[]{:S(2)}) copy-start(f32[1728]{0:T(1024)S(1)} %get-tuple-element.18) | copy-start | bytes 20740
  49.2 6.6 %copy-start.2 = (f32[1728]{0:T(1024)}, f32[1728]{0:T(1024)S(1)}, u32[]{:S(2)}) copy-start(f32[1728]{0:T(1024)S(1)} %get-tuple-element.19) | copy-start | bytes 20740
  55.7 334.2 %all-gather.5.cloned.1.call-start = ((), (), s32[]{:S(2)}) async-start(), calls=%async_computation.1 | async-start | bytes 22118400 | tf_op jit(solution)/shard_map/all_gather | solution.py:27
  389.9 17.7 %copy-start = (bf16[5120,1728]{0,1:T(8,128)(2,1)S(1)}, bf16[5120,1728]{0,1:T(8,128)(2,1)}, u32[]{:S(2)}) copy-start(bf16[5120,1728]{0,1:T(8,128)(2,1)} %all-gather.5.cloned.1.call-done) | copy-start | bytes 53084164
Sparse Core Ops, SparseCore 0:
  55.8 165.4 all-gather.2
  223.7 166.0 all-gather.4
where the time goes:
time: 421 us
  waiting for transfers between devices  327 us (78%)
  other arithmetic  37.7 us (9%)
  local copies, waits for them, and re-layouts  24.2 us (6%)
  blocking collectives  17.5 us (4%)
  between operations  14.1 us (3%)
    all_gather x1, waiting for transfers between devices, body(): lax.all_gather(narrow_up, 'zero', axis=0, tiled=True)  169 us
    all_gather x1, waiting for transfers between devices, body(): lax.all_gather(narrow_gate, 'zero', axis=0, tiled=True)  159 us
    reduce_max x1, other arithmetic, body(): jnp.max(jnp.abs(whole_gained_up), axis=0)  24.5 us
    unnamed x8, local copies, waits for them, and re-layouts  24.2 us
    pmax x1, blocking collectives, body(): lax.pmax((jnp.max(jnp.abs(whole_gained_gate), axis=0), jnp.max(jnp.abs(wh...  17.5 us
  transfers between devices with their start and end apart: 2, of which 2 were waited for; matrix products, arithmetic and copies ran while one was open for 2% of the time, Pallas kernels for 0%

commit v1 on v0

v1 whole, which is shorter than its diff:
```python
import jax
import jax.numpy as jnp
from jax import lax
from jax.experimental import pallas as pl
from jax.sharding import PartitionSpec as P


learn_rate = 0.3
hold_rate = 0.9
GATES = (5, 4, 6, 5)
LEADS = 2
UPS = (6, 6, 4, 2, 1)
unit = 8


def cuts_of(width, shares):
    edges, done = [0], 0
    for share in shares[:-1]:
        done += share
        edge = int(done / sum(shares) * width) // unit * unit
        if edges[-1] < edge < width:
            edges.append(edge)
    return list(zip(edges, edges[1:] + [width]))


def gained(train, drift, spread, gain, lo, hi):
    train, drift, spread = train[:, lo:hi], drift[:, lo:hi], spread[:, lo:hi]
    return (train - learn_rate * (hold_rate * drift + spread)) * gain[:, None]


def blank(*shape):
    return pl.pallas_call(
        lambda *refs: None,
        out_shape=[jax.ShapeDtypeStruct(shape, jnp.bfloat16)] * 2,
        out_specs=[pl.BlockSpec(memory_space=pl.ANY)] * 2,
    )()


def body_of(parts):
    def gather(narrow, out, lo):
        rows = narrow.shape[0]
        me = lax.axis_index("zero")

        def put(out, piece, owner, row=0):
            return lax.dynamic_update_slice(out, piece, (owner * rows + row, jnp.int32(lo)))

        if parts != 4:
            return lax.dynamic_update_slice(out, lax.all_gather(narrow, "zero", axis=0, tiled=True), (0, lo))

        def along(piece, side):
            return lax.ppermute(piece, "zero", [(i, i ^ side) for i in range(parts)])

        half = rows // 2
        first, second = along(narrow, 1), along(narrow, 2)
        far_top, far_bottom = along(first[:half], 2), along(second[half:], 1)
        out = put(out, narrow, me)
        out = put(out, first, me ^ 1)
        out = put(out, second, me ^ 2)
        out = put(out, far_top, me ^ 3)
        return put(out, far_bottom, me ^ 3, half)

    def largest(peaks):
        if parts != 4:
            return lax.pmax(peaks, "zero")
        sizes = [peak.shape[0] for peak in peaks]
        own = every = jnp.concatenate(peaks)
        for side in (1, 2, 3):
            other = lax.ppermute(own, "zero", [(i, i ^ side) for i in range(parts)])
            every = jnp.maximum(every, other)
        return [every[sum(sizes[:k]) : sum(sizes[: k + 1])] for k in range(len(sizes))]

    def body(train_gate, drift_gate, spread_gate, train_up, drift_up, spread_up, norm_gain):
        rows, width = train_gate.shape
        gate, up = (train_gate, drift_gate, spread_gate), (train_up, drift_up, spread_up)
        peak = lambda piece: jnp.max(jnp.abs(piece), axis=0)
        cuts = (cuts_of(width, GATES), cuts_of(width, UPS))
        lead = cuts[0][LEADS - 1][1]
        piece = gained(*gate, norm_gain, 0, lead)
        (factor_lead,) = largest((peak(piece),))
        narrow_lead = (piece / factor_lead).astype(jnp.bfloat16)
        *gate, token = lax.optimization_barrier((*gate, narrow_lead))
        *up, narrow_lead = lax.optimization_barrier((*up, token))
        rest_gate, rest_up = gained(*gate, norm_gain, lead, width), gained(*up, norm_gain, 0, width)
        factor_rest, factor_up = largest((peak(rest_gate), peak(rest_up)))
        scaled = lambda rest, factor, lo, hi: (rest[:, lo:hi] / factor[lo:hi]).astype(jnp.bfloat16)
        early = [narrow_lead[:, lo:hi] for lo, hi in cuts[0][:LEADS]]
        late = [scaled(rest_gate, factor_rest, lo - lead, hi - lead) for lo, hi in cuts[0][LEADS:]]
        late += [scaled(rest_up, factor_up, lo, hi) for lo, hi in cuts[1]]
        pieces = [*lax.optimization_barrier(early), *lax.optimization_barrier(late)]
        outs, turn = [], 0
        for ranges, out in zip(cuts, blank(width, rows * parts)):
            out = out.T
            for lo, _ in ranges:
                out = gather(pieces[turn], out, lo)
                turn += 1
            outs.append(out)
        factor_gate = jnp.concatenate([factor_lead, factor_rest])
        return (*outs, factor_gate, factor_up)

    return body


def solution(mesh):
    return jax.shard_map(
        body_of(mesh.shape["zero"]),
        mesh=mesh,
        in_specs=(
            P("zero", "width"),
            P("zero", "width"),
            P("zero", "width"),
            P("zero", "width"),
            P("zero", "width"),
            P("zero", "width"),
            P("zero"),
        ),
        out_specs=(P(None, "width"), P(None, "width"), P("width"), P("width")),
        check_vma=False,
    )
```

time: 421 us -> 343 us (0.81)
  waiting for transfers between devices: 327 us -> 191 us
  local copies, waits for them, and re-layouts: 24.2 us -> 77.1 us
  starting transfers between devices: 0.08 us -> 48 us
  blocking collectives: 17.5 us -> 0 us
  between operations: 14.1 us -> 1.03 us
  other arithmetic: 37.7 us -> 25.5 us
    all_gather x2 -> x0, waiting for transfers between devices: 327 us -> none  [the longest x1 169 us: body(): lax.all_gather(narrow_up, 'zero', axis=0, tiled=True)]
    ppermute x0 -> x42, waiting for transfers between devices: none -> 191 us  [the longest x36 185 us: along(): return lax.ppermute(piece, 'zero', [(i, i ^ side) for i in range(parts)])]
    dynamic_update_slice x0 -> x45, local copies, waits for them, and re-layouts: none -> 57.5 us  [put(): lax.dynamic_update_slice(out, piece, (owner * rows + row, jnp.int32(lo)))]
    ppermute x0 -> x42, starting transfers between devices: none -> 48 us  [the longest x36 39.8 us: along(): return lax.ppermute(piece, 'zero', [(i, i ^ side) for i in range(parts)])]
    unnamed x8 -> x52, local copies, waits for them, and re-layouts: 24.2 us -> 1.18 us
    slice x0 -> x28, local copies, waits for them, and re-layouts: none -> 18.4 us  [the longest x18 17.3 us: gather(): far_top, far_bottom = (along(first[:half], 2), along(second[half:], 1))]
    pmax x1 -> x0, blocking collectives: 17.5 us -> none  [body(): lax.pmax((jnp.max(jnp.abs(whole_gained_gate), axis=0), jnp.max(jnp.abs(wh...]
    convert_element_type x2 -> x7, other arithmetic: 13.2 us -> 3.33 us  [the longest x6 2.84 us: body(): (rest[:, lo:hi] / factor[lo:hi]).astype(jnp.bfloat16)]
  transfers between devices with their start and end apart: 2 -> 42, of which waited for: 2 -> 16; matrix products, arithmetic and copies ran while one was open for 2% -> 22% of each run, Pallas kernels for 0% -> 0%
where the time goes in v1:
time: 343 us; the launch traced here: 342 us
  waiting for transfers between devices  191 us (56%)
  local copies, waits for them, and re-layouts  77.1 us (22%)
  starting transfers between devices  48 us (14%)
  other arithmetic  25.5 us (7%)
    ppermute x36, waiting for transfers between devices, along(): return lax.ppermute(piece, 'zero', [(i, i ^ side) for i in range(parts)])  185 us
    dynamic_update_slice x45, local copies, waits for them, and re-layouts, put(): lax.dynamic_update_slice(out, piece, (owner * rows + row, jnp.int32(lo)))  57.5 us
    ppermute x36, starting transfers between devices, along(): return lax.ppermute(piece, 'zero', [(i, i ^ side) for i in range(parts)])  39.8 us
    reduce_max x3, other arithmetic, body(): peak = lambda piece: jnp.max(jnp.abs(piece), axis=0)  21.3 us
    slice x18, local copies, waits for them, and re-layouts, gather(): far_top, far_bottom = (along(first[:half], 2), along(second[half:], 1))  17.3 us
    ppermute x6, starting transfers between devices, largest(): other = lax.ppermute(own, 'zero', [(i, i ^ side) for i in range(parts)])  8.12 us
  transfers between devices with their start and end apart: 42, of which 16 were waited for; matrix products, arithmetic and copies ran while one was open for 22% of the time, Pallas kernels for 0%

profile of v1, /device:TPU:0, one launch (start us, length us, event | category | flops | bytes accessed | tf_op | source)
XLA Modules:
  0.0 342.2 jit_solution(8580340272812737908)
XLA Ops:
  0.6 5.5 %abs_reduce_fusion.2 = (f32[776]{0:T(1024)S(1)}, f32[1280,776]{0,1:T(8,128)S(1)}) fusion(f32[1280]{0:T(1024)} %param.13, f32[1280,1728]{0,1:T(8,128)} %param.9, f32[1280,1728]{0,1:T(8,128)} %param.8, f32[1280,1728]{0,1:T(8,128)} %param.7), kind=kLoop, calls=%fused_computation.5 | loop fusion | flops 6952184 | bytes 15900704 | tf_op jit(solution)/shard_map/reduce_max | solution.py:75
  6.2 4.0 %collective-permute-start.2 = (f32[776]{0:T(1024)S(1)}, f32[776]{0:T(1024)S(1)}, u32[]{:S(2)}, u32[]{:S(2)}) collective-permute-start(f32[776]{0:T(1024)S(1)} %get-tuple-element.46), channel_id=1, source_target_pairs={{0,24},{8,16},{16,8},{24,0},{1,25},{9,17},{17,9},{25,1},{2,26},{10... | collective-permute-start | bytes 9320 | tf_op jit(solution)/shard_map/ppermute | solution.py:68
  11.7 2.0 collective-permute-done.1
  14.8 5.9 %abs_reduce_fusion.1 = (f32[952]{0:T(1024)S(1)}, f32[1280,952]{0,1:T(8,128)S(1)}) fusion(f32[1280]{0:T(1024)S(1)} %copy-done.25, f32[1280,1728]{0,1:T(8,128)} %param.9, f32[1280,1728]{0,1:T(8,128)} %param.8, f32[1280,1728]{0,1:T(8,128)} %param.7), kind=kLoop, calls=%fused_computation.2 | loop fusion | flops 8528968 | bytes 19505888 | tf_op jit(solution)/shard_map/reduce_max | solution.py:75
  20.7 9.9 %abs_reduce_fusion = (f32[1728]{0:T(1024)S(1)}, f32[1280,1728]{0,1:T(8,128)S(1)}) fusion(f32[1280]{0:T(1024)S(1)} %copy-done.25, f32[1280,1728]{0,1:T(8,128)} %param.10, f32[1280,1728]{0,1:T(8,128)} %param.12, f32[1280,1728]{0,1:T(8,128)} %param.11), kind=kLoop, calls=%fused_computation | loop fusion | flops 15481152 | bytes 35401472 | tf_op jit(solution)/shard_map/reduce_max | solution.py:75
  39.3 2.0 collective-permute-start.38
  45.5 2.7 collective-permute-done.38
  48.2 1.9 collective-permute-start.7
  51.6 6.7 %collective-permute-done.34 = bf16[1280,184]{0,1:T(8,128)(2,1)S(1)} collective-permute-done((bf16[1280,184]{0,1:T(8,128)(2,1)S(1)}, bf16[1280,184]{0,1:T(8,128)(2,1)S(1)}, u32[]{:S(2)}, u32[]{:S(2)}) %collective-permute-start.34) | collective-permute-done | bytes 471072 | tf_op jit(solution)/shard_map/ppermute | solution.py:51
  58.3 1.9 collective-permute-start.35
  60.2 34.4 %collective-permute-done.35 = bf16[1280,184]{0,1:T(8,128)(2,1)S(1)} collective-permute-done((bf16[1280,184]{0,1:T(8,128)(2,1)S(1)}, bf16[1280,184]{0,1:T(8,128)(2,1)S(1)}, u32[]{:S(2)}, u32[]{:S(2)}) %collective-permute-start.35) | collective-permute-done | bytes 471072 | tf_op jit(solution)/shard_map/ppermute | solution.py:51
  99.1 51.5 %collective-permute-done.3 = bf16[1280,432]{0,1:T(8,128)(2,1)S(1)} collective-permute-done((bf16[1280,432]{0,1:T(8,128)(2,1)S(1)}, bf16[1280,432]{0,1:T(8,128)(2,1)S(1)}, u32[]{:S(2)}, u32[]{:S(2)}) %collective-permute-start.3) | collective-permute-done | bytes 1105952 | tf_op jit(solution)/shard_map/ppermute | solution.py:51
  150.8 1.9 collective-permute-start.23
  152.7 21.6 %collective-permute-done.18 = bf16[1280,432]{0,1:T(8,128)(2,1)S(1)} collective-permute-done((bf16[1280,432]{0,1:T(8,128)(2,1)S(1)}, bf16[1280,432]{0,1:T(8,128)(2,1)S(1)}, u32[]{:S(2)}, u32[]{:S(2)}) %collective-permute-start.18) | collective-permute-done | bytes 1105952 | tf_op jit(solution)/shard_map/ppermute | solution.py:51
  174.5 2.0 collective-permute-start.27
  178.5 2.5 constant_dynamic-update-slice_fusion.9
  193.7 2.3 constant_dynamic-update-slice_fusion.8
  196.0 2.3 constant_dynamic-update-slice_fusion.7
  199.7 36.4 %collective-permute-done.15 = bf16[1280,520]{0,1:T(8,128)(2,1)} collective-permute-done((bf16[1280,520]{0,1:T(8,128)(2,1)}, bf16[1280,520]{0,1:T(8,128)(2,1)}, u32[]{:S(2)}, u32[]{:S(2)}) %collective-permute-start.15) | collective-permute-done | bytes 1331232 | tf_op jit(solution)/shard_map/ppermute | solution.py:51
  247.6 2.5 constant_dynamic-update-slice_fusion.3
  250.2 2.5 constant_dynamic-update-slice_fusion.2
  252.7 8.2 %collective-permute-done.5 = bf16[640,432]{0,1:T(8,128)(2,1)S(1)} collective-permute-done((bf16[640,432]{0,1:T(8,128)(2,1)S(1)}, bf16[640,432]{0,1:T(8,128)(2,1)S(1)}, u32[]{:S(2)}, u32[]{:S(2)}) %collective-permute-start.5) | collective-permute-done | bytes 552992 | tf_op jit(solution)/shard_map/ppermute | solution.py:51
  266.3 2.1 constant_dynamic-update-slice_fusion.42
  272.3 2.5 constant_dynamic-update-slice_fusion.39
  275.9 2.5 constant_dynamic-update-slice_fusion.37
  278.5 9.4 %collective-permute-done.16 = bf16[640,520]{0,1:T(8,128)(2,1)S(1)} collective-permute-done((bf16[640,520]{0,1:T(8,128)(2,1)S(1)}, bf16[640,520]{0,1:T(8,128)(2,1)S(1)}, u32[]{:S(2)}, u32[]{:S(2)}) %collective-permute-start.16) | collective-permute-done | bytes 665632 | tf_op jit(solution)/shard_map/ppermute | solution.py:51
  298.6 7.7 %collective-permute-done.24 = bf16[640,544]{0,1:T(8,128)(2,1)S(1)} collective-permute-done((bf16[640,544]{0,1:T(8,128)(2,1)S(1)}, bf16[640,544]{0,1:T(8,128)(2,1)S(1)}, u32[]{:S(2)}, u32[]{:S(2)}) %collective-permute-start.24) | collective-permute-done | bytes 696352 | tf_op jit(solution)/shard_map/ppermute | solution.py:51
  311.1 2.5 constant_dynamic-update-slice_fusion.28
  313.6 2.5 constant_dynamic-update-slice_fusion.27
  316.2 6.6 %collective-permute-done.28 = bf16[640,544]{0,1:T(8,128)(2,1)S(1)} collective-permute-done((bf16[640,544]{0,1:T(8,128)(2,1)S(1)}, bf16[640,544]{0,1:T(8,128)(2,1)S(1)}, u32[]{:S(2)}, u32[]{:S(2)}) %collective-permute-start.28) | collective-permute-done | bytes 696352 | tf_op jit(solution)/shard_map/ppermute | solution.py:51
  327.3 2.2 constant_dynamic-update-slice_fusion.23
  329.4 2.2 constant_dynamic-update-slice_fusion.22
  (192 shorter events, 90.3 us)
Async XLA Ops:
  42.8 15.5 %collective-permute-start.34 = (bf16[1280,184]{0,1:T(8,128)(2,1)S(1)}, bf16[1280,184]{0,1:T(8,128)(2,1)S(1)}, u32[]{:S(2)}, u32[]{:S(2)}) collective-permute-start(bf16[1280,184]{0,1:T(8,128)(2,1)S(1)} %fusion.5), channel_id=1, source_target_pairs={{0,8},{8,0},{16,24},{24,16},{1,9},{9,1},{17,25},{25,17},{2,10},{10... | collective-permute-start | bytes 1413128 | tf_op jit(solution)/shard_map/ppermute | solution.py:51
  43.3 54.9 %collective-permute-start.30 = (bf16[1280,360]{0,1:T(8,128)(2,1)S(1)}, bf16[1280,360]{0,1:T(8,128)(2,1)}, u32[]{:S(2)}, u32[]{:S(2)}) collective-permute-start(bf16[1280,360]{0,1:T(8,128)(2,1)S(1)} %fusion.4), channel_id=1, source_target_pairs={{0,8},{8,0},{16,24},{24,16},{1,9},{9,1},{17,25},{25,17},{2,10},{10... | collective-permute-start | bytes 2764808 | tf_op jit(solution)/shard_map/ppermute | solution.py:51
  44.8 53.9 %collective-permute-start.31 = (bf16[1280,360]{0,1:T(8,128)(2,1)S(1)}, bf16[1280,360]{0,1:T(8,128)(2,1)}, u32[]{:S(2)}, u32[]{:S(2)}) collective-permute-start(bf16[1280,360]{0,1:T(8,128)(2,1)S(1)} %fusion.4), channel_id=1, source_target_pairs={{0,16},{8,24},{16,0},{24,8},{1,17},{9,25},{17,1},{25,9},{2,18},{10... | collective-permute-start | bytes 2764808 | tf_op jit(solution)/shard_map/ppermute | solution.py:51
  48.2 46.6 %collective-permute-start.7 = (bf16[1280,344]{0,1:T(8,128)(2,1)S(1)}, bf16[1280,344]{0,1:T(8,128)(2,1)S(1)}, u32[]{:S(2)}, u32[]{:S(2)}) collective-permute-start(bf16[1280,344]{0,1:T(8,128)(2,1)S(1)} %slice.137), channel_id=1, source_target_pairs={{0,8},{8,0},{16,24},{24,16},{1,9},{9,1},{17,25},{25,17},{2,10},{10... | collective-permute-start | bytes 2641928 | tf_op jit(solution)/shard_map/ppermute | solution.py:51
  50.1 46.6 %collective-permute-start.8 = (bf16[1280,344]{0,1:T(8,128)(2,1)S(1)}, bf16[1280,344]{0,1:T(8,128)(2,1)}, u32[]{:S(2)}, u32[]{:S(2)}) collective-permute-start(bf16[1280,344]{0,1:T(8,128)(2,1)S(1)} %slice.137), channel_id=1, source_target_pairs={{0,16},{8,24},{16,0},{24,8},{1,17},{9,25},{17,1},{25,9},{2,18},{10... | collective-permute-start | bytes 2641928 | tf_op jit(solution)/shard_map/ppermute | solution.py:51
  58.3 36.3 %collective-permute-start.35 = (bf16[1280,184]{0,1:T(8,128)(2,1)S(1)}, bf16[1280,184]{0,1:T(8,128)(2,1)S(1)}, u32[]{:S(2)}, u32[]{:S(2)}) collective-permute-start(bf16[1280,184]{0,1:T(8,128)(2,1)S(1)} %fusion.5), channel_id=1, source_target_pairs={{0,16},{8,24},{16,0},{24,8},{1,17},{9,25},{17,1},{25,9},{2,18},{10... | collective-permute-start | bytes 1413128 | tf_op jit(solution)/shard_map/ppermute | solution.py:51
  94.6 81.8 %collective-permute-start.14 = (bf16[1280,520]{0,1:T(8,128)(2,1)}, bf16[1280,520]{0,1:T(8,128)(2,1)S(1)}, u32[]{:S(2)}, u32[]{:S(2)}) collective-permute-start(bf16[1280,520]{0,1:T(8,128)(2,1)} %fusion.2), channel_id=1, source_target_pairs={{0,8},{8,0},{16,24},{24,16},{1,9},{9,1},{17,25},{25,17},{2,10},{10... | collective-permute-start | bytes 3993608 | tf_op jit(solution)/shard_map/ppermute | solution.py:51
  94.8 55.9 %collective-permute-start.3 = (bf16[1280,432]{0,1:T(8,128)(2,1)S(1)}, bf16[1280,432]{0,1:T(8,128)(2,1)S(1)}, u32[]{:S(2)}, u32[]{:S(2)}) collective-permute-start(bf16[1280,432]{0,1:T(8,128)(2,1)S(1)} %slice.136), channel_id=1, source_target_pairs={{0,8},{8,0},{16,24},{24,16},{1,9},{9,1},{17,25},{25,17},{2,10},{10... | collective-permute-start | bytes 3317768 | tf_op jit(solution)/shard_map/ppermute | solution.py:51
  96.7 54.1 %collective-permute-start.4 = (bf16[1280,432]{0,1:T(8,128)(2,1)S(1)}, bf16[1280,432]{0,1:T(8,128)(2,1)S(1)}, u32[]{:S(2)}, u32[]{:S(2)}) collective-permute-start(bf16[1280,432]{0,1:T(8,128)(2,1)S(1)} %slice.136), channel_id=1, source_target_pairs={{0,16},{8,24},{16,0},{24,8},{1,17},{9,25},{17,1},{25,9},{2,18},{10... | collective-permute-start | bytes 3317768 | tf_op jit(solution)/shard_map/ppermute | solution.py:51
  98.2 76.1 %collective-permute-start.18 = (bf16[1280,432]{0,1:T(8,128)(2,1)S(1)}, bf16[1280,432]{0,1:T(8,128)(2,1)S(1)}, u32[]{:S(2)}, u32[]{:S(2)}) collective-permute-start(bf16[1280,432]{0,1:T(8,128)(2,1)S(1)} %fusion.3), channel_id=1, source_target_pairs={{0,8},{8,0},{16,24},{24,16},{1,9},{9,1},{17,25},{25,17},{2,10},{10... | collective-permute-start | bytes 3317768 | tf_op jit(solution)/shard_map/ppermute | solution.py:51
  98.7 75.7 %collective-permute-start.19 = (bf16[1280,432]{0,1:T(8,128)(2,1)S(1)}, bf16[1280,432]{0,1:T(8,128)(2,1)S(1)}, u32[]{:S(2)}, u32[]{:S(2)}) collective-permute-start(bf16[1280,432]{0,1:T(8,128)(2,1)S(1)} %fusion.3), channel_id=1, source_target_pairs={{0,16},{8,24},{16,0},{24,8},{1,17},{9,25},{17,1},{25,9},{2,18},{10... | collective-permute-start | bytes 3317768 | tf_op jit(solution)/shard_map/ppermute | solution.py:51
  150.6 88.0 %collective-permute-start.22 = (bf16[1280,544]{0,1:T(8,128)(2,1)S(1)}, bf16[1280,544]{0,1:T(8,128)(2,1)}, u32[]{:S(2)}, u32[]{:S(2)}) collective-permute-start(bf16[1280,544]{0,1:T(8,128)(2,1)S(1)} %get-tuple-element.37), channel_id=1, source_target_pairs={{0,8},{8,0},{16,24},{24,16},{1,9},{9,1},{17,25},{25,17},{2,10},{10... | collective-permute-start | bytes 4177928 | tf_op jit(solution)/shard_map/ppermute | solution.py:51
  150.8 89.8 %collective-permute-start.23 = (bf16[1280,544]{0,1:T(8,128)(2,1)S(1)}, bf16[1280,544]{0,1:T(8,128)(2,1)}, u32[]{:S(2)}, u32[]{:S(2)}) collective-permute-start(bf16[1280,544]{0,1:T(8,128)(2,1)S(1)} %get-tuple-element.37), channel_id=1, source_target_pairs={{0,16},{8,24},{16,0},{24,8},{1,17},{9,25},{17,1},{25,9},{2,18},{10... | collective-permute-start | bytes 4177928 | tf_op jit(solution)/shard_map/ppermute | solution.py:51
  174.3 67.9 %collective-permute-start.26 = (bf16[1280,544]{0,1:T(8,128)(2,1)S(1)}, bf16[1280,544]{0,1:T(8,128)(2,1)}, u32[]{:S(2)}, u32[]{:S(2)}) collective-permute-start(bf16[1280,544]{0,1:T(8,128)(2,1)S(1)} %get-tuple-element.38), channel_id=1, source_target_pairs={{0,8},{8,0},{16,24},{24,16},{1,9},{9,1},{17,25},{25,17},{2,10},{10... | collective-permute-start | bytes 4177928 | tf_op jit(solution)/shard_map/ppermute | solution.py:51
  174.5 70.3 %collective-permute-start.27 = (bf16[1280,544]{0,1:T(8,128)(2,1)S(1)}, bf16[1280,544]{0,1:T(8,128)(2,1)}, u32[]{:S(2)}, u32[]{:S(2)}) collective-permute-start(bf16[1280,544]{0,1:T(8,128)(2,1)S(1)} %get-tuple-element.38), channel_id=1, source_target_pairs={{0,16},{8,24},{16,0},{24,8},{1,17},{9,25},{17,1},{25,9},{2,18},{10... | collective-permute-start | bytes 4177928 | tf_op jit(solution)/shard_map/ppermute | solution.py:51
  177.6 58.5 %collective-permute-start.15 = (bf16[1280,520]{0,1:T(8,128)(2,1)}, bf16[1280,520]{0,1:T(8,128)(2,1)}, u32[]{:S(2)}, u32[]{:S(2)}) collective-permute-start(bf16[1280,520]{0,1:T(8,128)(2,1)} %fusion.2), channel_id=1, source_target_pairs={{0,16},{8,24},{16,0},{24,8},{1,17},{9,25},{17,1},{25,9},{2,18},{10... | collective-permute-start | bytes 3993608 | tf_op jit(solution)/shard_map/ppermute | solution.py:51
  236.1 104.7 %collective-permute-start.40 = (bf16[640,96]{0,1:T(8,128)(2,1)S(1)}, bf16[640,96]{0,1:T(8,128)(2,1)S(1)}, u32[]{:S(2)}, u32[]{:S(2)}) collective-permute-start(bf16[640,96]{0,1:T(8,128)(2,1)S(1)} %slice.205), channel_id=1, source_target_pairs={{0,16},{8,24},{16,0},{24,8},{1,17},{9,25},{17,1},{25,9},{2,18},{10... | collective-permute-start | bytes 368648 | tf_op jit(solution)/shard_map/ppermute | solution.py:51
  238.6 29.8 %collective-permute-start.9 = (bf16[640,344]{0,1:T(8,128)(2,1)S(1)}, bf16[640,344]{0,1:T(8,128)(2,1)S(1)}, u32[]{:S(2)}, u32[]{:S(2)}) collective-permute-start(bf16[640,344]{0,1:T(8,128)(2,1)S(1)} %slice.177), channel_id=1, source_target_pairs={{0,16},{8,24},{16,0},{24,8},{1,17},{9,25},{17,1},{25,9},{2,18},{10... | collective-permute-start | bytes 1320968 | tf_op jit(solution)/shard_map/ppermute | solution.py:51
  240.5 29.4 %collective-permute-start.10 = (bf16[640,344]{0,1:T(8,128)(2,1)S(1)}, bf16[640,344]{0,1:T(8,128)(2,1)S(1)}, u32[]{:S(2)}, u32[]{:S(2)}) collective-permute-start(bf16[640,344]{0,1:T(8,128)(2,1)S(1)} %slice.178), channel_id=1, source_target_pairs={{0,8},{8,0},{16,24},{24,16},{1,9},{9,1},{17,25},{25,17},{2,10},{10... | collective-permute-start | bytes 1320968 | tf_op jit(solution)/shard_map/ppermute | solution.py:51
  242.2 18.7 %collective-permute-start.5 = (bf16[640,432]{0,1:T(8,128)(2,1)S(1)}, bf16[640,432]{0,1:T(8,128)(2,1)S(1)}, u32[]{:S(2)}, u32[]{:S(2)}) collective-permute-start(bf16[640,432]{0,1:T(8,128)(2,1)S(1)} %slice.175), channel_id=1, source_target_pairs={{0,16},{8,24},{16,0},{24,8},{1,17},{9,25},{17,1},{25,9},{2,18},{10... | collective-permute-start | bytes 1658888 | tf_op jit(solution)/shard_map/ppermute | solution.py:51
  244.8 18.3 %collective-permute-start.6 = (bf16[640,432]{0,1:T(8,128)(2,1)S(1)}, bf16[640,432]{0,1:T(8,128)(2,1)S(1)}, u32[]{:S(2)}, u32[]{:S(2)}) collective-permute-start(bf16[640,432]{0,1:T(8,128)(2,1)S(1)} %slice.176), channel_id=1, source_target_pairs={{0,8},{8,0},{16,24},{24,16},{1,9},{9,1},{17,25},{25,17},{2,10},{10... | collective-permute-start | bytes 1658888 | tf_op jit(solution)/shard_map/ppermute | solution.py:51
  260.9 33.7 %collective-permute-start.20 = (bf16[640,432]{0,1:T(8,128)(2,1)S(1)}, bf16[640,432]{0,1:T(8,128)(2,1)S(1)}, u32[]{:S(2)}, u32[]{:S(2)}) collective-permute-start(bf16[640,432]{0,1:T(8,128)(2,1)S(1)} %slice.195), channel_id=1, source_target_pairs={{0,16},{8,24},{16,0},{24,8},{1,17},{9,25},{17,1},{25,9},{2,18},{10... | collective-permute-start | bytes 1658888 | tf_op jit(solution)/shard_map/ppermute | solution.py:51
  263.1 34.0 %collective-permute-start.21 = (bf16[640,432]{0,1:T(8,128)(2,1)S(1)}, bf16[640,432]{0,1:T(8,128)(2,1)S(1)}, u32[]{:S(2)}, u32[]{:S(2)}) collective-permute-start(bf16[640,432]{0,1:T(8,128)(2,1)S(1)} %slice.196), channel_id=1, source_target_pairs={{0,8},{8,0},{16,24},{24,16},{1,9},{9,1},{17,25},{25,17},{2,10},{10... | collective-permute-start | bytes 1658888 | tf_op jit(solution)/shard_map/ppermute | solution.py:51
  268.5 19.4 %collective-permute-start.16 = (bf16[640,520]{0,1:T(8,128)(2,1)S(1)}, bf16[640,520]{0,1:T(8,128)(2,1)S(1)}, u32[]{:S(2)}, u32[]{:S(2)}) collective-permute-start(bf16[640,520]{0,1:T(8,128)(2,1)S(1)} %slice.193), channel_id=1, source_target_pairs={{0,16},{8,24},{16,0},{24,8},{1,17},{9,25},{17,1},{25,9},{2,18},{10... | collective-permute-start | bytes 1996808 | tf_op jit(solution)/shard_map/ppermute | solution.py:51
  269.9 20.2 %collective-permute-start.17 = (bf16[640,520]{0,1:T(8,128)(2,1)S(1)}, bf16[640,520]{0,1:T(8,128)(2,1)S(1)}, u32[]{:S(2)}, u32[]{:S(2)}) collective-permute-start(bf16[640,520]{0,1:T(8,128)(2,1)S(1)} %slice.194), channel_id=1, source_target_pairs={{0,8},{8,0},{16,24},{24,16},{1,9},{9,1},{17,25},{25,17},{2,10},{10... | collective-permute-start | bytes 1996808 | tf_op jit(solution)/shard_map/ppermute | solution.py:51
  287.9 18.5 %collective-permute-start.24 = (bf16[640,544]{0,1:T(8,128)(2,1)S(1)}, bf16[640,544]{0,1:T(8,128)(2,1)S(1)}, u32[]{:S(2)}, u32[]{:S(2)}) collective-permute-start(bf16[640,544]{0,1:T(8,128)(2,1)S(1)} %slice.197), channel_id=1, source_target_pairs={{0,16},{8,24},{16,0},{24,8},{1,17},{9,25},{17,1},{25,9},{2,18},{10... | collective-permute-start | bytes 2088968 | tf_op jit(solution)/shard_map/ppermute | solution.py:51
  290.1 18.5 %collective-permute-start.25 = (bf16[640,544]{0,1:T(8,128)(2,1)S(1)}, bf16[640,544]{0,1:T(8,128)(2,1)S(1)}, u32[]{:S(2)}, u32[]{:S(2)}) collective-permute-start(bf16[640,544]{0,1:T(8,128)(2,1)S(1)} %slice.198), channel_id=1, source_target_pairs={{0,8},{8,0},{16,24},{24,16},{1,9},{9,1},{17,25},{25,17},{2,10},{10... | collective-permute-start | bytes 2088968 | tf_op jit(solution)/shard_map/ppermute | solution.py:51
  294.6 46.9 %collective-permute-start.41 = (bf16[640,96]{0,1:T(8,128)(2,1)S(1)}, bf16[640,96]{0,1:T(8,128)(2,1)S(1)}, u32[]{:S(2)}, u32[]{:S(2)}) collective-permute-start(bf16[640,96]{0,1:T(8,128)(2,1)S(1)} %slice.206), channel_id=1, source_target_pairs={{0,8},{8,0},{16,24},{24,16},{1,9},{9,1},{17,25},{25,17},{2,10},{10... | collective-permute-start | bytes 368648 | tf_op jit(solution)/shard_map/ppermute | solution.py:51
  297.1 40.2 %collective-permute-start.36 = (bf16[640,184]{0,1:T(8,128)(2,1)S(1)}, bf16[640,184]{0,1:T(8,128)(2,1)S(1)}, u32[]{:S(2)}, u32[]{:S(2)}) collective-permute-start(bf16[640,184]{0,1:T(8,128)(2,1)S(1)} %slice.203), channel_id=1, source_target_pairs={{0,16},{8,24},{16,0},{24,8},{1,17},{9,25},{17,1},{25,9},{2,18},{10... | collective-permute-start | bytes 706568 | tf_op jit(solution)/shard_map/ppermute | solution.py:51
  306.3 16.4 %collective-permute-start.28 = (bf16[640,544]{0,1:T(8,128)(2,1)S(1)}, bf16[640,544]{0,1:T(8,128)(2,1)S(1)}, u32[]{:S(2)}, u32[]{:S(2)}) collective-permute-start(bf16[640,544]{0,1:T(8,128)(2,1)S(1)} %slice.199), channel_id=1, source_target_pairs={{0,16},{8,24},{16,0},{24,8},{1,17},{9,25},{17,1},{25,9},{2,18},{10... | collective-permute-start | bytes 2088968 | tf_op jit(solution)/shard_map/ppermute | solution.py:51
  308.6 16.4 %collective-permute-start.29 = (bf16[640,544]{0,1:T(8,128)(2,1)S(1)}, bf16[640,544]{0,1:T(8,128)(2,1)S(1)}, u32[]{:S(2)}, u32[]{:S(2)}) collective-permute-start(bf16[640,544]{0,1:T(8,128)(2,1)S(1)} %slice.200), channel_id=1, source_target_pairs={{0,8},{8,0},{16,24},{24,16},{1,9},{9,1},{17,25},{25,17},{2,10},{10... | collective-permute-start | bytes 2088968 | tf_op jit(solution)/shard_map/ppermute | solution.py:51
  325.0 9.1 %collective-permute-start.33 = (bf16[640,360]{0,1:T(8,128)(2,1)S(1)}, bf16[640,360]{0,1:T(8,128)(2,1)S(1)}, u32[]{:S(2)}, u32[]{:S(2)}) collective-permute-start(bf16[640,360]{0,1:T(8,128)(2,1)S(1)} %slice.202), channel_id=1, source_target_pairs={{0,8},{8,0},{16,24},{24,16},{1,9},{9,1},{17,25},{25,17},{2,10},{10... | collective-permute-start | bytes 1382408 | tf_op jit(solution)/shard_map/ppermute | solution.py:51
  (36 other events, 1561.0 us)
